TPU v7x, 32 devices: a whole 2x2x4 slice. The times are simulated.
32 devices in a mesh: views: 2 (over x), depth: 16 (over z, y, core).
Axes of the slice: x: 2, y: 2, z: 4, core: 2. Of those that a mesh axis runs over, the one named last changes fastest.
Arguments:
- density: float32 [512, 128, 256], P(('views', 'depth')), parts along dimension 0, may hold values from 0.2 to 5
- emission: bfloat16 [6, 256, 128, 256], P('views', 'depth'), parts along dimension 0, may hold values from 0 to 1
- occupancy: int32 [32, 4, 4], P(('views', 'depth')), parts along dimension 0, may hold values 0 or 1
- facing: int32 [2], P('views'), parts along dimension 0, may hold values from 0 to 1
Outputs:
- image: float32 [8, 128, 256], P('views', 'depth'), parts along dimension 0
There are 2 independent parts, one for each index of `views`. A program takes and returns all parts, laid end to end along the dimension named above; each array names one. Nothing has to cross between parts.
Inputs may be any that keep to these rules, and one draw needn't show every extreme that they name: `occupancy`: 1 where the tile of the brick is occupied; where it is 0 the tile's cells neither absorb nor emit. `facing`: 0: bricks and cells of lower depth index are nearer the camera; 1: those of higher index.
All inputs are finite; a program needn't handle non-finite values. No bound on the sum of `occupancy` on one device may be relied on, other than what follows from the above.
Results may differ from a plain program's by a relative error of at most 0.0003.
Values sent between devices are 32-bit elements; how exact they have to be, the bound alone decides.
A program may use at most 128 MiB of HBM per device.

v0:
```python
import jax
import jax.numpy as jnp
from jax import lax
from jax.sharding import PartitionSpec as P


def march(dense, emitted, occupied, facing, bricks):
    depth_len, height, width = dense.shape
    tiles_h, tiles_w = occupied.shape
    gating = occupied.astype(jnp.float32)[None, :, None, :, None]
    optical = (
        dense.reshape(depth_len, tiles_h, height // tiles_h, tiles_w, width // tiles_w) * gating
    ).reshape(dense.shape) / (depth_len * bricks)
    column = jnp.cumsum(optical, axis=0)
    whole = column[-1]
    ahead = jnp.where(facing == 0, column - optical, whole[None] - column)
    weight = (1.0 - jnp.exp(-optical)) * jnp.exp(-ahead)
    radiance = jnp.sum(emitted.astype(jnp.float32) * weight[None], axis=1)
    return (radiance, jnp.exp(-whole))


def composite(radiance, transmit, facing):
    ones_row = jnp.ones_like(transmit[:1])
    forward = jnp.cumprod(transmit, axis=0)
    ahead_forward = jnp.concatenate([ones_row, forward[:-1]], axis=0)
    backward = jnp.flip(jnp.cumprod(jnp.flip(transmit, 0), axis=0), 0)
    ahead_backward = jnp.concatenate([backward[1:], ones_row], axis=0)
    front = jnp.where(facing == 0, ahead_forward, ahead_backward)
    colour = jnp.sum(radiance * front, axis=0)
    opacity = 1.0 - forward[-1]
    return jnp.concatenate([colour, opacity], axis=0)


def on_device(density, emission, occupancy, facing):
    bricks = lax.axis_size("depth")
    facing_now = facing[0]
    radiance, transmit = march(density, emission, occupancy[0], facing_now, bricks)
    every_colour, every_transmit = (
        lax.all_to_all(radiance[None], "depth", split_axis=2, concat_axis=0, tiled=True),
        lax.all_to_all(transmit[None, None], "depth", split_axis=2, concat_axis=0, tiled=True),
    )
    return composite(every_colour, every_transmit, facing_now)


def solution(mesh):
    return jax.shard_map(
        on_device,
        mesh=mesh,
        in_specs=(
            P(("views", "depth"), None, None),
            P("views", "depth", None, None),
            P(("views", "depth"), None, None),
            P("views"),
        ),
        out_specs=P("views", "depth", None),
        check_vma=False,
    )
```

profile of v0, /device:TPU:0, one launch (start us, length us, event | category | flops | bytes accessed | tf_op | source)
XLA Modules:
  0.0 35.3 jit_solution(3524464965204813712)
XLA Ops:
  0.0 0.7 %convert_bitcast_fusion = f32[4,4]{1,0:T(4,128)S(1)} fusion(s32[1,4,4]{2,1,0:T(4,128)} %param.6), kind=kLoop, calls=%fused_computation.14 | loop fusion | flops 16 | bytes 128 | tf_op jit(solution)/shard_map/convert_element_type | solution.py:10
  0.7 0.1 mul.37
  0.8 0.2 mul.38
  1.0 1.8 %fusion = f32[16,128,256]{2,1,0:T(8,128)S(1)} fusion(f32[16,128,256]{2,1,0:T(8,128)} %param.4, f32[128,256]{1,0:T(8,128)S(1)} %mul.38), kind=kOutput, calls=%fused_computation.3 | output fusion | flops 8912896 | bytes 4325376 | tf_op jit(solution)/shard_map/jit(cumsum)/reduce_window_sum | solution.py:14
  2.8 0.8 %copy.18 = f32[1,1,128,256]{3,1,0,2:T(1,128)} copy(f32[1,1,128,256]{3,2,1,0:T(8,128)S(1)} %get-tuple-element.6) | data formatting | bytes 262144 | tf_op jit(solution)/shard_map/exp | solution.py:19
  3.6 7.4 %all-to-all-start.1 = ((f32[1,1,128,256]{3,1,0,2:T(1,128)}), f32[1,1,128,256]{3,1,0,2:T(1,128)S(1)}, u32[]{:S(2)}, u32[]{:S(2)}) async-start(f32[1,1,128,256]{3,1,0,2:T(1,128)} %copy.18), calls=%async_computation.1 | async-start | bytes 262144 | tf_op jit(solution)/shard_map/all_to_all | solution.py:40
  11.7 0.0 copy-start
  11.7 2.6 %exponential_multiply_fusion = f32[16,128,256]{2,1,0:T(8,128)S(1)} fusion(f32[16,128,256]{2,1,0:T(8,128)S(1)} %fusion, f32[16,128,256]{2,1,0:T(8,128)} %param.4, f32[128,256]{1,0:T(8,128)S(1)} %get-tuple-element.5, f32[128,256]{1,0:T(8,128)S(1)} %mul.38, pred[]{:T(512)} %bitcast.1), kind=kLoop, calls=%fused_computation.1 | loop fusion | flops 4718592 | bytes 6553601 | tf_op jit(solution)/shard_map/mul | solution.py:17
  14.3 0.0 copy-done
  14.3 0.6 %multiply_reduce_fusion = f32[3,128,256]{2,1,0:T(8,128)S(1)} fusion(bf16[3,16,128,256]{3,2,1,0:T(8,128)(2,1)S(1)} %copy-done, f32[16,128,256]{2,1,0:T(8,128)S(1)} %exponential_multiply_fusion), kind=kLoop, calls=%fused_computation | loop fusion | flops 4620288 | bytes 5636096 | tf_op jit(solution)/shard_map/reduce_sum | solution.py:18
  14.9 1.1 %copy.16 = f32[1,3,128,256]{3,0,1,2:T(1,128)} copy(f32[1,3,128,256]{3,2,1,0:T(8,128)S(1)} %bitcast.22) | data formatting | bytes 786432 | tf_op jit(solution)/shard_map/broadcast_in_dim | solution.py:39
  16.1 2.9 %all-to-all-done.1 = f32[1,1,128,256]{3,1,0,2:T(1,128)S(1)} async-done(((f32[1,1,128,256]{3,1,0,2:T(1,128)}), f32[1,1,128,256]{3,1,0,2:T(1,128)S(1)}, u32[]{:S(2)}, u32[]{:S(2)}) %all-to-all-start.1) | async-done | bytes 131104 | tf_op jit(solution)/shard_map/all_to_all | solution.py:40
  18.9 3.6 %all-to-all-start = ((f32[1,3,128,256]{3,0,1,2:T(1,128)}), f32[1,3,128,256]{3,0,1,2:T(1,128)S(1)}, u32[]{:S(2)}, u32[]{:S(2)}) async-start(f32[1,3,128,256]{3,0,1,2:T(1,128)} %copy.16), calls=%async_computation | async-start | bytes 786432 | tf_op jit(solution)/shard_map/all_to_all | solution.py:39
  22.5 1.4 %fusion.8 = f32[16,1,8,256]{3,2,1,0:T(8,128)S(1)} fusion(f32[16,1,8,256]{3,2,1,0:T(8,128)S(1)} %rev.5), kind=kOutput, calls=%fused_computation.18 | output fusion | flops 491520 | bytes 262144 | tf_op jit(solution)/shard_map/jit(cumprod)/reduce_window | solution.py:26
  23.9 0.1 fusion.6
  24.1 10.5 %all-to-all-done = f32[1,3,128,256]{3,0,1,2:T(1,128)S(1)} async-done(((f32[1,3,128,256]{3,0,1,2:T(1,128)}), f32[1,3,128,256]{3,0,1,2:T(1,128)S(1)}, u32[]{:S(2)}, u32[]{:S(2)}) %all-to-all-start) | async-done | bytes 393248 | tf_op jit(solution)/shard_map/all_to_all | solution.py:39
  34.7 0.6 %copy.23 = f32[4,8,256]{2,1,0:T(8,128)} copy(f32[4,8,256]{2,0,1:T(4,128)S(1)} %pad_maximum_fusion) | data formatting | bytes 65536 | tf_op jit(solution)/shard_map/concatenate | solution.py:31
  (12 shorter events, 0.2 us)
Async XLA Ops:
  3.6 15.3 %all-to-all-start.1 = ((f32[1,1,128,256]{3,1,0,2:T(1,128)}), f32[1,1,128,256]{3,1,0,2:T(1,128)S(1)}, u32[]{:S(2)}, u32[]{:S(2)}) async-start(f32[1,1,128,256]{3,1,0,2:T(1,128)} %copy.18), calls=%async_computation.1 | async-start | bytes 262144 | tf_op jit(solution)/shard_map/all_to_all | solution.py:40
  11.7 2.6 %copy-start = (bf16[3,16,128,256]{3,2,1,0:T(8,128)(2,1)S(1)}, bf16[3,16,128,256]{3,2,1,0:T(8,128)(2,1)}, u32[]{:S(2)}) copy-start(bf16[3,16,128,256]{3,2,1,0:T(8,128)(2,1)} %param.5) | copy-start | bytes 9437188
  18.9 15.7 %all-to-all-start = ((f32[1,3,128,256]{3,0,1,2:T(1,128)}), f32[1,3,128,256]{3,0,1,2:T(1,128)S(1)}, u32[]{:S(2)}, u32[]{:S(2)}) async-start(f32[1,3,128,256]{3,0,1,2:T(1,128)} %copy.16), calls=%async_computation | async-start | bytes 786432 | tf_op jit(solution)/shard_map/all_to_all | solution.py:39
where the time goes:
time: 35.7 us; the launch traced here: 35.3 us
  waiting for transfers between devices  13.4 us (38%)
  starting transfers between devices  11 us (31%)
  other arithmetic  7.24 us (20%)
  local copies, waits for them, and re-layouts  2.94 us (8%)
  between operations  0.8 us (2%)
    all_to_all x1, waiting for transfers between devices, on_device(): lax.all_to_all(radiance[None], 'depth', split_axis=2, concat_axis=0, tile...  10.5 us
    all_to_all x1, starting transfers between devices, on_device(): lax.all_to_all(transmit[None, None], 'depth', split_axis=2, concat_axis=0...  7.41 us
    all_to_all x1, starting transfers between devices, on_device(): lax.all_to_all(radiance[None], 'depth', split_axis=2, concat_axis=0, tile...  3.55 us
    all_to_all x1, waiting for transfers between devices, on_device(): lax.all_to_all(transmit[None, None], 'depth', split_axis=2, concat_axis=0...  2.87 us
    mul x1, other arithmetic, march(): weight = (1.0 - jnp.exp(-optical)) * jnp.exp(-ahead)  2.56 us
    another operation x1, other arithmetic, march(): column = jnp.cumsum(optical, axis=0)  1.8 us
    another operation x1, other arithmetic, composite(): backward = jnp.flip(jnp.cumprod(jnp.flip(transmit, 0), axis=0), 0)  1.37 us
    broadcast_in_dim x1, local copies, waits for them, and re-layouts, on_device(): radiance[None]  1.14 us
  transfers between devices with their start and end apart: 2, of which 2 were waited for; matrix products, arithmetic and copies ran while one was open for 17% of the time, Pallas kernels for 0%

commit v1 on v0

v1 whole, which is shorter than its diff:
```python
import functools
import math

import jax
import jax.numpy as jnp
from jax import lax
from jax.experimental import pallas as pl
from jax.experimental.pallas import tpu as pltpu
from jax.sharding import PartitionSpec as P

MESH = pl.DeviceIdType.MESH
STEP_ROWS = 16


def over(mine, theirs, mine_near):
    keep = mine_near + (1.0 - mine_near) * theirs[3]
    gain = (1.0 - mine_near) + mine_near * mine[3]
    colour = mine[:3] * keep[None] + theirs[:3] * gain[None]
    return colour, mine[3] * theirs[3]


def kernel(
    n, occ_ref, facing_ref, dens_hbm, emis_hbm, out_ref,
    dens, emis, loc, got1, pair, got2, quad, got3,
    dens_sem, emis_sem, send1, recv1, send2, recv2, send3, recv3,
):
    groups = n // 4
    depth_len, height, width = dens_hbm.shape
    rows = height // groups
    tile = rows // 4
    tiles_h, tiles_w = occ_ref.shape[1:]
    tile_rows, tile_cols = height // tiles_h, width // tiles_w
    step = min(STEP_ROWS, rows)

    me = lax.axis_index("depth")
    core = lax.rem(me, 2)
    side = lax.rem(me // 2, 2)
    group = me // 4
    core_peer = group * 4 + side * 2 + (1 - core)
    side_peer = group * 4 + (1 - side) * 2 + core

    def target(k):
        if k == groups - 1:
            return group
        down = jnp.where(groups - 1 - k > group, groups - 1 - k, groups - 2 - k)
        up = jnp.where(k < group, k, k + 1)
        return jnp.where(group < groups // 2, down, up)

    targets = [target(k) for k in range(groups)]
    loads = []
    for k in range(groups):
        span = pl.ds(pl.multiple_of(targets[k] * rows, rows), rows)
        loads.append((
            pltpu.make_async_copy(dens_hbm.at[:, span, :], dens.at[k], dens_sem.at[k]),
            pltpu.make_async_copy(emis_hbm.at[:, :, span, :], emis.at[k], emis_sem.at[k]),
        ))
    for load in loads:
        load[0].start()
        load[1].start()

    barrier = pltpu.get_barrier_semaphore()
    peers = [core_peer, side_peer]
    for off in range(1, groups):
        peers.append(lax.rem(group + off, groups) * 4 + side * 2 + core)
    for peer in peers:
        pl.semaphore_signal(barrier, inc=1, device_id={"depth": peer}, device_id_type=MESH)

    flip = facing_ref[0].astype(jnp.float32)
    sign = 1.0 - 2.0 * flip
    base = -math.log2(math.e) / (depth_len * n)
    col_tile = lax.broadcasted_iota(jnp.int32, (1, width), 1) // tile_cols

    def march(k):
        loads[k][0].wait()
        loads[k][1].wait()
        for row0 in range(0, rows, step):
            tile_row = (targets[k] * rows + row0) // tile_rows
            gate = jnp.zeros((1, width), jnp.float32)
            for i in range(tiles_w):
                gate = jnp.where(col_tile == i, occ_ref[0, tile_row, i].astype(jnp.float32), gate)
            scale = jnp.broadcast_to(gate * base, (step, width))
            cells = [dens[k, z, row0:row0 + step, :] for z in range(depth_len)]
            total = cells[0]
            for z in range(1, depth_len):
                total = total + cells[z]
            total = total * scale
            level = total * flip
            signed = scale * sign
            glow = jnp.exp2(level)
            sums = [jnp.zeros((step, width), jnp.float32) for _ in range(3)]
            for z in range(depth_len):
                level = level + signed * cells[z]
                later = jnp.exp2(level)
                weight = glow - later
                glow = later
                for c in range(3):
                    sums[c] = sums[c] + emis[k, c, z, row0:row0 + step, :].astype(jnp.float32) * weight
            planes = [s * sign for s in sums] + [jnp.exp2(total)]
            for t in range(step // tile):
                spot = row0 // tile + t
                for c in range(4):
                    loc[k, spot % 2, spot // 2, c] = planes[c][t * tile:(t + 1) * tile]

    def copy1(k):
        return pltpu.make_async_remote_copy(
            src_ref=loc.at[k, 1 - core], dst_ref=got1.at[k],
            send_sem=send1.at[k], recv_sem=recv1.at[k],
            device_id={"depth": core_peer}, device_id_type=MESH)

    def copy2(k):
        return pltpu.make_async_remote_copy(
            src_ref=pair.at[k, 1 - side], dst_ref=got2.at[k],
            send_sem=send2.at[k], recv_sem=recv2.at[k],
            device_id={"depth": side_peer}, device_id_type=MESH)

    def copy3(k):
        return pltpu.make_async_remote_copy(
            src_ref=quad.at[k], dst_ref=got3.at[group],
            send_sem=send3.at[k], recv_sem=recv3.at[group],
            device_id={"depth": targets[k] * 4 + side * 2 + core}, device_id_type=MESH)

    core_near = 1.0 - jnp.abs(core.astype(jnp.float32) - flip)
    side_near = 1.0 - jnp.abs(side.astype(jnp.float32) - flip)

    def merge1(k):
        copy1(k).wait_recv()
        for s in range(2):
            colour, clear = over(loc[k, core, s], got1[k, s], core_near)
            pair[k, s, :3] = colour
            pair[k, s, 3] = clear
        copy2(k).start()

    def merge2(k):
        copy2(k).wait_recv()
        colour, clear = over(pair[k, side], got2[k], side_near)
        if k == groups - 1:
            got3[group, :3] = colour
            got3[group, 3] = clear
        else:
            quad[k, :3] = colour
            quad[k, 3] = clear
            copy3(k).start()

    for k in range(groups):
        march(k)
        if k == 0:
            pl.semaphore_wait(barrier, len(peers))
        copy1(k).start()
        if k >= 2:
            merge1(k - 2)
    for k in range(max(groups - 2, 0), groups):
        merge1(k)
    for k in range(groups):
        merge2(k)

    for off in range(1, groups):
        source = lax.rem(group + off, groups)
        pltpu.make_async_remote_copy(
            src_ref=quad.at[0], dst_ref=got3.at[source],
            send_sem=send3.at[0], recv_sem=recv3.at[source],
            device_id={"depth": core_peer}, device_id_type=MESH).wait_recv()
    colour, clear = got3[0, :3], got3[0, 3]
    for g in range(1, groups):
        more, more_clear = got3[g, :3], got3[g, 3]
        keep = (1.0 - flip) + flip * more_clear
        gain = flip + (1.0 - flip) * clear
        colour = colour * keep[None] + more * gain[None]
        clear = clear * more_clear
    out_ref[:3] = colour
    out_ref[3] = 1.0 - clear

    for k in range(groups):
        copy1(k).wait_send()
        copy2(k).wait_send()
        if k < groups - 1:
            copy3(k).wait_send()


def on_device(n, density, emission, occupancy, facing):
    depth_len, height, width = density.shape
    groups = n // 4
    rows = height // groups
    tile = rows // 4
    smem = pl.BlockSpec(memory_space=pltpu.SMEM)
    hbm = pl.BlockSpec(memory_space=pl.ANY)
    dma = pltpu.SemaphoreType.DMA((groups,))
    return pl.pallas_call(
        functools.partial(kernel, n),
        out_shape=jax.ShapeDtypeStruct((4, tile, width), jnp.float32),
        in_specs=[smem, smem, hbm, hbm],
        out_specs=pl.BlockSpec(memory_space=pltpu.VMEM),
        scratch_shapes=[
            pltpu.VMEM((groups, depth_len, rows, width), density.dtype),
            pltpu.VMEM((groups, 3, depth_len, rows, width), emission.dtype),
            pltpu.VMEM((groups, 2, 2, 4, tile, width), jnp.float32),
            pltpu.VMEM((groups, 2, 4, tile, width), jnp.float32),
            pltpu.VMEM((groups, 2, 4, tile, width), jnp.float32),
            pltpu.VMEM((groups, 4, tile, width), jnp.float32),
            pltpu.VMEM((groups, 4, tile, width), jnp.float32),
            pltpu.VMEM((groups, 4, tile, width), jnp.float32),
        ] + [dma] * 8,
        compiler_params=pltpu.CompilerParams(collective_id=0, has_side_effects=True),
        name="render",
    )(occupancy, facing, density, emission)


def solution(mesh):
    return jax.shard_map(
        functools.partial(on_device, mesh.shape["depth"]),
        mesh=mesh,
        in_specs=(
            P(("views", "depth"), None, None),
            P("views", "depth", None, None),
            P(("views", "depth"), None, None),
            P("views"),
        ),
        out_specs=P("views", "depth", None),
        check_vma=False,
    )
```

time: 35.7 us -> 17.5 us (0.49)
  Pallas kernels: 0 us -> 15.3 us
  waiting for transfers between devices: 13.4 us -> 0 us
  starting transfers between devices: 11 us -> 0 us
  other arithmetic: 7.24 us -> 0 us
  local copies, waits for them, and re-layouts: 2.94 us -> 1.38 us
    pallas_call x0 -> x1, Pallas kernels: none -> 15.3 us  [on_device(): pl.pallas_call(functools.partial(kernel, n), out_shape=jax.ShapeDtypeStru...]
    all_to_all x2 -> x0, waiting for transfers between devices: 13.4 us -> none  [the longest x1 10.5 us: on_device(): lax.all_to_all(radiance[None], 'depth', split_axis=2, concat_axis=0, tile...]
    all_to_all x2 -> x0, starting transfers between devices: 11 us -> none  [the longest x1 7.41 us: on_device(): lax.all_to_all(transmit[None, None], 'depth', split_axis=2, concat_axis=0...]
    another operation x3 -> x0, other arithmetic: 3.24 us -> none  [the longest x1 1.8 us: march(): column = jnp.cumsum(optical, axis=0)]
    mul x2 -> x0, other arithmetic: 2.59 us -> none  [the longest x1 2.56 us: march(): weight = (1.0 - jnp.exp(-optical)) * jnp.exp(-ahead)]
    unnamed x3 -> x1, local copies, waits for them, and re-layouts: 0.02 us -> 1.38 us
    broadcast_in_dim x1 -> x0, local copies, waits for them, and re-layouts: 1.14 us -> none  [on_device(): radiance[None]]
    exp x1 -> x0, local copies, waits for them, and re-layouts: 0.79 us -> none  [march(): return (radiance, jnp.exp(-whole))]
  transfers between devices with their start and end apart: 2 -> 0, of which waited for: 2 -> 0; matrix products, arithmetic and copies ran while one was open for 17% -> 0% of each run, Pallas kernels for 0% -> 0%
where the time goes in v1:
time: 17.5 us; the launch traced here: 17.3 us
  Pallas kernels  15.3 us (87%)
  local copies, waits for them, and re-layouts  1.38 us (8%)
  between operations  0.66 us (4%)
    pallas_call x1, Pallas kernels, on_device(): pl.pallas_call(functools.partial(kernel, n), out_shape=jax.ShapeDtypeStru...  15.3 us
    unnamed x1, local copies, waits for them, and re-layouts  1.38 us

profile of v1, /device:TPU:0, one launch (start us, length us, event | category | flops | bytes accessed | tf_op | source)
XLA Modules:
  0.0 17.3 jit_solution(1463767711944405247)
XLA Ops:
  0.7 15.3 %render.1 = f32[4,8,256]{2,1,0:T(8,128)} custom-call(s32[1,4,4]{2,1,0:T(4,128)} %occ_ref.1, s32[1]{0:T(128)S(6)} %copy.6.facing_ref, f32[16,128,256]{2,1,0:T(8,128)} %dens_hbm.1, bf16[3,16,128,256]{3,2,1,0:T(8,128)(2,1)} %emis_hbm.1), custom_call_target="tpu_custom_call" | custom-call | tf_op jit(solution)/shard_map/render/pallas_call | solution.py:187
  15.9 1.4 %copy.7 = f32[4,8,256]{2,1,0:T(8,128)} copy(f32[4,8,256]{2,1,0:T(8,128)} %render.1) | data formatting | bytes 65536
